TPU v7x, 128 devices: a whole 4x4x4 slice. The times are simulated.
128 devices in a mesh: obs: 4 (over z), face: 32 (over x, y, core).
Axes of the slice: x: 4, y: 4, z: 4, core: 2. Of those that a mesh axis runs over, the one named last changes fastest.
Arguments:
- density: float32 [34, 32768], P(None, ('obs', 'face')), may hold values from 0.6 to 1.4
- velocity: float32 [3, 34, 32768], P(None, None, ('obs', 'face')), may hold values from -6 to 6
- pressure: float32 [34, 32768], P(None, ('obs', 'face')), may hold values from -6 to 6
- normal: float32 [3, 32768], P(None, ('obs', 'face')), may hold values from -1 to 1, as said below
- direction: float32 [128, 32, 3], P(('obs', 'face')), may hold values from -1 to 1, as said below
- weights: bfloat16 [128, 32, 768, 256], P(('obs', 'face')), may hold values from -0.21875 to 0.21875
- bin_index: int32 [128, 32], P(('obs', 'face')), may hold values from 0 to 31, as said below
- group_index: int32 [128, 32], P(('obs', 'face')), may hold values from 0 to 3
- item_count: int32 [128], P(('obs', 'face')), may hold values from 16 to 32, as said below
Outputs:
- signal: float32 [1024, 1024], P('face', 'obs')
Inputs may be any that keep to these rules, and one draw needn't show every extreme that they name: `bin_index`: no time block is named more than 2 times in one device's list; in every draw some device names a block 2 times among its live entries. `item_count`: some device has all 32 entries live. Each face's normal has unit length. Each entry's direction has unit length.
All inputs are finite; a program needn't handle non-finite values.
Results may differ from a plain program's by a relative error of at most 0.0029.
Values sent between devices are 32-bit elements; how exact they have to be, the bound alone decides.
No kernel may reach another device: no remote copies, remote signals or barrier semaphores. Data moves between devices by JAX's collectives and lax.ppermute only.
A program may use at most 64 MiB of HBM per device.

v0:
```python
import jax
import jax.numpy as jnp
from jax import lax
from jax.sharding import PartitionSpec as P

SLOT_CAP = 2


def in_blocks(array, dim, count):
    before, after = (array.shape[:dim], array.shape[dim + 1 :])
    return jnp.moveaxis(array.reshape(*before, count, -1, *after), dim, 0)


def sum_at_owner(array, axis, dim):
    parts = in_blocks(array, dim, lax.axis_size(axis))
    arrived = lax.all_to_all(parts, axis, split_axis=0, concat_axis=0, tiled=True)
    return arrived.sum(axis=0)


def face_terms(dens, veloc, press, norms):
    normal_speed = veloc[0] * norms[0][None] + veloc[1] * norms[1][None] + veloc[2] * norms[2][None]
    flux = dens * normal_speed
    load_first = press * norms[0][None] + dens * veloc[0] * normal_speed
    load_second = press * norms[1][None] + dens * veloc[1] * normal_speed
    load_third = press * norms[2][None] + dens * veloc[2] * normal_speed
    thick = 0.5 * (flux[2:] - flux[:-2])
    return (thick, load_first, load_second, load_third)


def item_source(thick, load_first, load_second, load_third, heading):
    radial = heading[0] * load_first + heading[1] * load_second + heading[2] * load_third
    rate = 0.5 * (radial[2:] - radial[:-2])
    return jnp.concatenate([thick, rate, radial[1:-1]], axis=1).astype(jnp.bfloat16)


def local(
    density, velocity, pressure, normal, direction, weights, bin_index, group_index, item_count
):
    thick, load_first, load_second, load_third = face_terms(density, velocity, pressure, normal)
    headings = direction[0]
    matrices = weights[0]
    blocks_of = bin_index[0]
    groups_of = group_index[0]
    live_count = item_count[0]
    list_total = matrices.shape[0]
    steps = thick.shape[0]
    width = matrices.shape[2]
    n_face = lax.axis_size("face")
    n_obs = lax.axis_size("obs")

    def item_block(listed):
        heading = lax.dynamic_index_in_dim(headings, listed, 0, False)
        source = item_source(thick, load_first, load_second, load_third, heading)
        matrix = lax.dynamic_index_in_dim(matrices, listed, 0, False)
        return jnp.dot(source, matrix, preferred_element_type=jnp.float32)

    order = jnp.arange(list_total, dtype=jnp.int32)
    is_live = order < live_count
    matches = (
        (blocks_of[:, None] == blocks_of[None, :])
        & (order[:, None] > order[None, :])
        & is_live[None, :]
    )
    slot_index = blocks_of * SLOT_CAP + jnp.sum(matches.astype(jnp.int32), axis=1)

    def add_routed(listed, carried):
        outgoing, labels = carried
        target = slot_index[listed]
        outgoing = lax.dynamic_update_index_in_dim(outgoing, item_block(listed)[None], target, 0)
        labels = labels.at[target].set(groups_of[listed].astype(jnp.float32))
        return (outgoing, labels)

    empty_blocks = jnp.zeros((n_face * SLOT_CAP, steps, width), jnp.float32)
    empty_labels = jnp.zeros((n_face * SLOT_CAP,), jnp.float32)
    outgoing, labels = lax.fori_loop(0, live_count, add_routed, (empty_blocks, empty_labels))
    arrived, arrived_labels = (
        lax.all_to_all(
            outgoing.reshape(n_face, SLOT_CAP, steps, width),
            "face",
            split_axis=0,
            concat_axis=0,
            tiled=True,
        ),
        lax.all_to_all(
            labels.reshape(n_face, SLOT_CAP), "face", split_axis=0, concat_axis=0, tiled=True
        ),
    )
    selector = (
        arrived_labels.reshape(1, -1) == jnp.arange(n_obs, dtype=jnp.float32)[:, None]
    ).astype(jnp.float32)
    grouped = jnp.dot(
        selector,
        arrived.reshape(n_face * SLOT_CAP, steps * width),
        precision=lax.Precision.HIGHEST,
        preferred_element_type=jnp.float32,
    )
    owned = sum_at_owner(grouped.reshape(n_obs, steps, width), "obs", 0)
    return owned.reshape(steps, width)


def solution(mesh):
    placed = (
        P(None, ("obs", "face")),
        P(None, None, ("obs", "face")),
        P(None, ("obs", "face")),
        P(None, ("obs", "face")),
        P(("obs", "face"), None, None),
        P(("obs", "face"), None, None, None),
        P(("obs", "face"), None),
        P(("obs", "face"), None),
        P(("obs", "face")),
    )
    return jax.shard_map(
        local, mesh=mesh, in_specs=placed, out_specs=P("face", "obs"), check_vma=False
    )
```

profile of v0, /device:TPU:0, one launch (start us, length us, event | category | flops | bytes accessed | tf_op | source)
XLA Modules:
  0.0 286.1 jit_solution(10141828849065942715)
XLA Ops:
  5.8 164.5 %while.14 = (s32[]{:T(128)}, f32[64,32,256]{2,1,0:T(8,128)S(1)}, f32[64]{0:T(128)S(1)}, s32[]{:T(128)}, bf16[32,256]{1,0:T(8,128)(2,1)S(1)}, /*index=5*/f32[32,3...) while((s32[]{:T(128)}, f32[64,32,256]{2,1,0:T(8,128)S(1)}, ...), condition=%wide.wide.region_2.3_spmd, body=%wide.wide.region_1.2_spmd.sunk | while | flops 12798477 | bytes 729951 | solution.py:75
  7.1 1.8 multiply_add_fusion.3
  13.9 1.8 multiply_add_fusion.3
  20.7 1.8 multiply_add_fusion.3
  27.6 1.8 multiply_add_fusion.3
  34.4 1.8 multiply_add_fusion.3
  41.2 1.8 multiply_add_fusion.3
  48.1 1.8 multiply_add_fusion.3
  54.9 1.8 multiply_add_fusion.3
  61.7 1.8 multiply_add_fusion.3
  68.5 1.8 multiply_add_fusion.3
  75.4 1.8 multiply_add_fusion.3
  82.2 1.8 multiply_add_fusion.3
  89.0 1.8 multiply_add_fusion.3
  95.9 1.8 multiply_add_fusion.3
  102.7 1.8 multiply_add_fusion.3
  109.5 1.8 multiply_add_fusion.3
  116.3 1.8 multiply_add_fusion.3
  123.2 1.8 multiply_add_fusion.3
  170.4 67.5 %all_to_all.19 = f32[32,1,2]{2,1,0:T(1,128)S(1)} all-to-all(f32[32,1,2]{2,1,0:T(1,128)S(1)} %bitcast.95), channel_id=1, replica_groups=mesh['obs'=4,'face'=32] {'face'}, dimensions={0} | all-to-all | bytes 512 | tf_op jit(solution)/shard_map/all_to_all | solution.py:84
  237.9 4.0 %all-to-all-start.1 = ((f32[32,2,32,256]{3,2,1,0:T(8,128)}), f32[32,2,32,256]{3,2,1,0:T(8,128)S(1)}, u32[]{:S(2)}, u32[]{:S(2)}) async-start(f32[32,2,32,256]{3,2,1,0:T(8,128)} %bitcast.92), calls=%async_computation.1 | async-start | bytes 4194304 | tf_op jit(solution)/shard_map/all_to_all | solution.py:77
  243.3 27.6 %all-to-all-done.1 = f32[32,2,32,256]{3,2,1,0:T(8,128)S(1)} async-done(((f32[32,2,32,256]{3,2,1,0:T(8,128)}), f32[32,2,32,256]{3,2,1,0:T(8,128)S(1)}, u32[]{:S(2)}, u32[]{:S(2)}) %all-to-all-start.1) | async-done | bytes 2097184 | tf_op jit(solution)/shard_map/all_to_all | solution.py:77
  270.9 2.0 fusion.15
  272.9 12.6 %all_to_all.20 = f32[4,1,32,256]{3,2,1,0:T(8,128)S(1)} all-to-all(f32[4,1,32,256]{3,2,1,0:T(8,128)S(1)} %copy.16), channel_id=1, replica_groups=mesh['obs'=4,'face'=32] {'obs'}, dimensions={0} | all-to-all | bytes 262144 | tf_op jit(solution)/shard_map/all_to_all | solution.py:16
  (194 shorter events, 80.4 us)
Async XLA Ops:
  0.0 5.8 %copy-start.1 = (s32[1,32]{1,0:T(1,128)S(1)}, s32[1,32]{1,0:T(1,128)}, u32[]{:S(2)}) copy-start(s32[1,32]{1,0:T(1,128)} %param.20) | copy-start | bytes 388
  170.3 67.7 %copy-start = (f32[64,32,256]{2,1,0:T(8,128)}, f32[64,32,256]{2,1,0:T(8,128)S(1)}, u32[]{:S(2)}) copy-start(f32[64,32,256]{2,1,0:T(8,128)S(1)} %get-tuple-element.82) | copy-start | bytes 6291460
  237.9 32.9 %all-to-all-start.1 = ((f32[32,2,32,256]{3,2,1,0:T(8,128)}), f32[32,2,32,256]{3,2,1,0:T(8,128)S(1)}, u32[]{:S(2)}, u32[]{:S(2)}) async-start(f32[32,2,32,256]{3,2,1,0:T(8,128)} %bitcast.92), calls=%async_computation.1 | async-start | bytes 4194304 | tf_op jit(solution)/shard_map/all_to_all | solution.py:77
where the time goes:
time: 290 us; the launch traced here: 286 us
  blocking collectives  80.2 us (28%)
  loops' own time  58.2 us (20%)
  other arithmetic  53.2 us (18%)
  local copies, waits for them, and re-layouts  32.5 us (11%)
  matrix products  29.7 us (10%)
  waiting for transfers between devices  27.6 us (10%)
  starting transfers between devices  4.01 us (1%)
    all_to_all x1, blocking collectives, local(): lax.all_to_all(labels.reshape(n_face, SLOT_CAP), 'face', split_axis=0, co...  67.5 us
    another operation x1, loops' own time, local(): lax.fori_loop(0, live_count, add_routed, (empty_blocks, empty_labels))  58.2 us
    add x24, other arithmetic, item_source(): heading[0] * load_first + heading[1] * load_second + heading[2] * load_third  44 us
    dot_general x24, matrix products, item_block(): return jnp.dot(source, matrix, preferred_element_type=jnp.float32)  27.7 us
    all_to_all x1, waiting for transfers between devices, local(): lax.all_to_all(outgoing.reshape(n_face, SLOT_CAP, steps, width), 'face',...  27.6 us
    slice x24, local copies, waits for them, and re-layouts, item_source(): heading[0] * load_first + heading[1] * load_second + heading[2] * load_third  14.1 us
    dynamic_slice x24, local copies, waits for them, and re-layouts, add_routed(): target = slot_index[listed]  14 us
    all_to_all x1, blocking collectives, sum_at_owner(): lax.all_to_all(parts, axis, split_axis=0, concat_axis=0, tiled=True)  12.6 us
  transfers between devices with their start and end apart: 1, of which 1 were waited for; matrix products, arithmetic and copies ran while one was open for 0% of the time, Pallas kernels for 0%

commit v1 on v0

v1 whole, which is shorter than its diff:
```python
import jax
import jax.numpy as jnp
from jax import lax
from jax.experimental import pallas as pl
from jax.experimental.pallas import tpu as pltpu
from jax.sharding import PartitionSpec as P

SLOT_CAP = 2
DEPTH = 8
UNROLL = 2


def item_kernel(
    bins, groups, count, headings, dens, veloc, press, norms, matrices,
    outgoing, labels, ring, linear, thick, slots, named, sems,
):
    list_total, _, width = matrices.shape[1:]
    live = count[0]

    def fetch(listed):
        spot = lax.rem(listed, DEPTH)
        return pltpu.make_async_copy(matrices.at[0, listed], ring.at[spot], sems.at[spot])

    for listed in range(DEPTH):
        @pl.when(listed < live)
        def _():
            fetch(listed).start()

    faces = dens.shape[1]
    face_terms(dens, veloc, press, norms, linear, thick)
    outgoing[...] = jnp.zeros_like(outgoing)

    def clear(block, carry):
        named[block] = 0
        labels[block * SLOT_CAP] = 0.0
        labels[block * SLOT_CAP + 1] = 0.0
        return carry

    lax.fori_loop(0, named.shape[0], clear, 0)

    def place(listed, carry):
        block = bins[0, listed]
        target = block * SLOT_CAP + named[block]
        named[block] = named[block] + 1
        slots[listed] = target
        labels[target] = groups[0, listed].astype(jnp.float32)
        return carry

    lax.fori_loop(0, live, place, 0)

    def step(turn, carry):
        for part in range(UNROLL):
            listed = turn * UNROLL + part

            @pl.when(listed < live)
            def _():
                fetch(listed).wait()

        for part in range(UNROLL):
            listed = turn * UNROLL + part
            valid = listed < live
            known = jnp.where(valid, listed, 0)
            spot = lax.rem(listed, DEPTH)
            mixed = (
                headings[0, 0, known] * linear[0]
                + headings[1, 0, known] * linear[1]
                + headings[2, 0, known] * linear[2]
            ).astype(jnp.bfloat16)
            source = jnp.concatenate([thick[...], mixed], axis=1)
            block = jnp.dot(source, ring[spot], preferred_element_type=jnp.float32)
            target = slots[known]
            outgoing[target] = jnp.where(valid, block, outgoing[target])

        for part in range(UNROLL):
            listed = turn * UNROLL + part + DEPTH

            @pl.when(listed < live)
            def _():
                fetch(listed).start()

        return carry

    lax.fori_loop(0, pl.cdiv(live, UNROLL), step, 0)


def face_terms(dens, veloc, press, norms, linear, thick):
    faces = dens.shape[1]
    across = [norms[axis : axis + 1, :] for axis in range(3)]
    moving = [veloc[axis] for axis in range(3)]
    density = dens[...]
    pressure = press[...]
    normal_speed = moving[0] * across[0] + moving[1] * across[1] + moving[2] * across[2]
    flux = density * normal_speed
    thick[...] = (0.5 * (flux[2:] - flux[:-2])).astype(jnp.bfloat16)
    for axis in range(3):
        load = pressure * across[axis] + density * moving[axis] * normal_speed
        linear[axis, :, :faces] = 0.5 * (load[2:] - load[:-2])
        linear[axis, :, faces:] = load[1:-1]


def local(
    density, velocity, pressure, normal, direction, weights, bin_index, group_index, item_count
):
    n_face = lax.axis_size("face")
    n_obs = lax.axis_size("obs")
    list_total, depth, width = weights.shape[1:]
    steps = density.shape[0] - 2
    faces = density.shape[1]
    headings = direction.transpose(2, 0, 1)
    smem = pl.BlockSpec(memory_space=pltpu.SMEM)
    vmem = pl.BlockSpec(memory_space=pltpu.VMEM)
    outgoing, labels = pl.pallas_call(
        item_kernel,
        out_shape=(
            jax.ShapeDtypeStruct((n_face * SLOT_CAP, steps, width), jnp.float32),
            jax.ShapeDtypeStruct((n_face * SLOT_CAP,), jnp.float32),
        ),
        in_specs=[smem, smem, smem, smem, vmem, vmem, vmem, vmem, pl.BlockSpec(memory_space=pl.ANY)],
        out_specs=(vmem, smem),
        scratch_shapes=[
            pltpu.VMEM((DEPTH, depth, width), jnp.bfloat16),
            pltpu.VMEM((3, steps, 2 * faces), jnp.float32),
            pltpu.VMEM((steps, faces), jnp.bfloat16),
            pltpu.SMEM((list_total,), jnp.int32),
            pltpu.SMEM((n_face,), jnp.int32),
            pltpu.SemaphoreType.DMA((DEPTH,)),
        ],
        name="items",
    )(bin_index, group_index, item_count, headings, density, velocity, pressure, normal, weights)
    arrived, arrived_labels = (
        lax.all_to_all(
            outgoing.reshape(n_face, SLOT_CAP, steps, width),
            "face",
            split_axis=0,
            concat_axis=0,
            tiled=True,
        ),
        lax.all_to_all(
            labels.reshape(n_face, SLOT_CAP), "face", split_axis=0, concat_axis=0, tiled=True
        ),
    )
    selector = (
        arrived_labels.reshape(1, -1) == jnp.arange(n_obs, dtype=jnp.float32)[:, None]
    ).astype(jnp.float32)
    grouped = jnp.dot(
        selector,
        arrived.reshape(n_face * SLOT_CAP, steps * width),
        precision=lax.Precision.HIGHEST,
        preferred_element_type=jnp.float32,
    )
    grouped = grouped.reshape(n_obs, steps, width)
    arrived = lax.all_to_all(grouped, "obs", split_axis=0, concat_axis=0, tiled=True)
    return arrived.sum(axis=0)


def solution(mesh):
    placed = (
        P(None, ("obs", "face")),
        P(None, None, ("obs", "face")),
        P(None, ("obs", "face")),
        P(None, ("obs", "face")),
        P(("obs", "face"), None, None),
        P(("obs", "face"), None, None, None),
        P(("obs", "face"), None),
        P(("obs", "face"), None),
        P(("obs", "face")),
    )
    return jax.shard_map(
        local, mesh=mesh, in_specs=placed, out_specs=P("face", "obs"), check_vma=False
    )
```

time: 290 us -> 71.1 us (0.25); the launches traced: 286 us -> 70.6 us
  loops' own time: 58.2 us -> 0 us
  blocking collectives: 80.2 us -> 25.3 us
  other arithmetic: 53.2 us -> 1.31 us
  local copies, waits for them, and re-layouts: 32.5 us -> 1.39 us
  matrix products: 29.7 us -> 1.96 us
  Pallas kernels: 0 us -> 8.33 us
    another operation x1 -> x0, loops' own time: 58.2 us -> none  [local(): lax.fori_loop(0, live_count, add_routed, (empty_blocks, empty_labels))]
    all_to_all x1, blocking collectives: 67.5 us -> 14.4 us  [local(): lax.all_to_all(labels.reshape(n_face, SLOT_CAP), 'face', split_axis=0, co...]
    add x27 -> x0, other arithmetic: 46.4 us -> none  [the longest x24 44 us: item_source(): heading[0] * load_first + heading[1] * load_second + heading[2] * load_third]
    dot_general x24 -> x0, matrix products: 27.7 us -> none  [item_block(): return jnp.dot(source, matrix, preferred_element_type=jnp.float32)]
    dynamic_slice x48 -> x0, local copies, waits for them, and re-layouts: 15.8 us -> none  [the longest x24 14 us: add_routed(): target = slot_index[listed]]
    slice x49 -> x0, local copies, waits for them, and re-layouts: 15.1 us -> none  [the longest x24 14.1 us: item_source(): heading[0] * load_first + heading[1] * load_second + heading[2] * load_third]
    pallas_call x0 -> x1, Pallas kernels: none -> 8.33 us  [local(): pl.pallas_call(item_kernel, out_shape=(jax.ShapeDtypeStruct((n_face * SLO...]
    scatter x24 -> x0, other arithmetic: 4.32 us -> none  [add_routed(): labels = labels.at[target].set(groups_of[listed].astype(jnp.float32))]
  transfers between devices with their start and end apart: 1 -> 1, of which waited for: 1 -> 1; matrix products, arithmetic and copies ran while one was open for 0% -> 2% of each run, Pallas kernels for 0% -> 0%
where the time goes in v1:
time: 71.1 us; the launch traced here: 70.6 us
  waiting for transfers between devices  27.6 us (39%)
  blocking collectives  25.3 us (36%)
  Pallas kernels  8.33 us (12%)
  starting transfers between devices  4.01 us (6%)
  matrix products  1.96 us (3%)
  local copies, waits for them, and re-layouts  1.39 us (2%)
  other arithmetic  1.31 us (2%)
    all_to_all x1, waiting for transfers between devices, local(): lax.all_to_all(outgoing.reshape(n_face, SLOT_CAP, steps, width), 'face',...  27.6 us
    all_to_all x1, blocking collectives, local(): lax.all_to_all(labels.reshape(n_face, SLOT_CAP), 'face', split_axis=0, co...  14.4 us
    all_to_all x1, blocking collectives, local(): lax.all_to_all(grouped, 'obs', split_axis=0, concat_axis=0, tiled=True)  10.9 us
    pallas_call x1, Pallas kernels, local(): pl.pallas_call(item_kernel, out_shape=(jax.ShapeDtypeStruct((n_face * SLO...  8.33 us
    all_to_all x1, starting transfers between devices, local(): lax.all_to_all(outgoing.reshape(n_face, SLOT_CAP, steps, width), 'face',...  4.01 us
    dot_general x1, matrix products, local(): jnp.dot(selector, arrived.reshape(n_face * SLOT_CAP, steps * width), prec...  1.96 us
  transfers between devices with their start and end apart: 1, of which 1 were waited for; matrix products, arithmetic and copies ran while one was open for 2% of the time, Pallas kernels for 0%

profile of v1, /device:TPU:0, one launch (start us, length us, event | category | flops | bytes accessed | tf_op | source)
XLA Modules:
  0.0 70.6 jit_solution(3579603114682412976)
XLA Ops:
  0.7 8.3 %items.1 = (f32[64,32,256]{2,1,0:T(8,128)}, f32[64]{0:T(128)}) custom-call(s32[1,32]{1,0:T(1,128)} %bins.1, s32[1,32]{1,0:T(1,128)} %groups.1, s32[1]{0:T(128)S(6)} %copy.23.count, f32[3,1,32]{2,1,0:T(1,128)} %bitcast.21, f32[34,256]{1,0:T(8,128)} %dens.1, f32[3,34,256]{2,1,0:T(8,128)} %veloc.1, f32[34,256]{1,0:T(8,128)} %press.1, f32[3,256]{1,0:T(4,128)} %norms.1, ...), custom_call_target="tpu_custom_call" | custom-call | tf_op jit(solution)/shard_map/items/pallas_call | solution.py:112
  9.0 0.8 %all_to_all.12 = f32[32,1,2]{2,0,1:T(8,128)S(1)} reshape(f32[64]{0:T(128)} %get-tuple-element.7) | data formatting | bytes 512 | tf_op jit(solution)/shard_map/all_to_all | solution.py:138
  9.8 14.4 %all_to_all.19 = f32[32,1,2]{2,1,0:T(1,128)S(1)} all-to-all(f32[32,1,2]{2,1,0:T(1,128)S(1)} %bitcast.20), channel_id=1, replica_groups=mesh['obs'=4,'face'=32] {'face'}, dimensions={0} | all-to-all | bytes 512 | tf_op jit(solution)/shard_map/all_to_all | solution.py:138
  24.2 4.0 %all-to-all-start.1 = ((f32[32,2,32,256]{3,2,1,0:T(8,128)}), f32[32,2,32,256]{3,2,1,0:T(8,128)S(1)}, u32[]{:S(2)}, u32[]{:S(2)}) async-start(f32[32,2,32,256]{3,2,1,0:T(8,128)} %bitcast.19), calls=%async_computation.1 | async-start | bytes 4194304 | tf_op jit(solution)/shard_map/all_to_all | solution.py:131
  28.2 0.5 broadcast.3
  28.7 0.7 reduce.3
  29.4 0.1 eq.15
  29.5 27.6 %all-to-all-done.1 = f32[32,2,32,256]{3,2,1,0:T(8,128)S(1)} async-done(((f32[32,2,32,256]{3,2,1,0:T(8,128)}), f32[32,2,32,256]{3,2,1,0:T(8,128)S(1)}, u32[]{:S(2)}, u32[]{:S(2)}) %all-to-all-start.1) | async-done | bytes 2097184 | tf_op jit(solution)/shard_map/all_to_all | solution.py:131
  57.1 2.0 %fusion = f32[4,32,256]{2,0,1:T(4,128)S(1)} fusion(f32[64]{0:T(128)S(1)} %eq.15, f32[8,8,32,256]{3,2,1,0:T(8,128)S(1)} %bitcast.18), kind=kOutput, calls=%fused_computation | convolution fusion | flops 25166080 | bytes 2228480 | tf_op jit(solution)/shard_map/dot_general | solution.py:145
  59.1 10.9 %all_to_all.20 = f32[4,32,256]{2,1,0:T(8,128)S(1)} all-to-all(f32[4,32,256]{2,1,0:T(8,128)S(1)} %copy.13), channel_id=1, replica_groups=mesh['obs'=4,'face'=32] {'obs'}, dimensions={0} | all-to-all | bytes 262144 | tf_op jit(solution)/shard_map/all_to_all | solution.py:152
  70.0 0.6 reduce_sum.9
  (1 shorter events, 0.0 us)
Async XLA Ops:
  24.2 32.9 %all-to-all-start.1 = ((f32[32,2,32,256]{3,2,1,0:T(8,128)}), f32[32,2,32,256]{3,2,1,0:T(8,128)S(1)}, u32[]{:S(2)}, u32[]{:S(2)}) async-start(f32[32,2,32,256]{3,2,1,0:T(8,128)} %bitcast.19), calls=%async_computation.1 | async-start | bytes 4194304 | tf_op jit(solution)/shard_map/all_to_all | solution.py:131
